TPU v7x, 128 devices: a whole 4x4x4 slice. The times are simulated.
128 devices in a mesh: tp: 16 (over z, y), dp: 8 (over x, core).
Axes of the slice: x: 4, y: 4, z: 4, core: 2. Of those that a mesh axis runs over, the one named last changes fastest.
Arguments:
- hidden: bfloat16 [16, 512, 1536], P('dp')
- gamma: float32 [1536], replicated
- w_head: bfloat16 [1536, 151936], P(None, 'tp')
- labels: int32 [16, 512], P('dp')
- mask: int32 [16, 512], P('dp')
Outputs:
- output 1: float32 [], replicated
- output 2: bfloat16 [16, 512, 1536], P('dp')
- output 3: float32 [1536, 151936], P(None, 'tp')
- output 4: float32 [1536], replicated
All inputs are finite; a program needn't handle non-finite values.
Results may differ from a plain program's by a relative error of at most 0.001.
Values sent between devices are 32-bit elements.
A program may use at most 1 GiB of HBM per device.

v0:
```python
import jax
import jax.numpy as jnp
from jax import lax
from jax.sharding import PartitionSpec as P

EPS = 1e-5


def solution(mesh):
    def local_step(hidden, gamma, w_head, labels, mask):
        num_seqs, seqlen, dmodel = hidden.shape
        vocab_local = w_head.shape[1]
        tokens = num_seqs * seqlen
        tok_rows = hidden.reshape(tokens, dmodel).astype(jnp.float32)
        inv_rms = lax.rsqrt(jnp.mean(tok_rows * tok_rows, axis=-1, keepdims=True) + EPS)
        normed = tok_rows * inv_rms
        unit_rows = (normed * gamma).astype(jnp.bfloat16)
        logits = jnp.dot(unit_rows, w_head, preferred_element_type=jnp.float32)
        local_ids = labels.reshape(tokens) - lax.axis_index("tp") * vocab_local
        is_label = local_ids[:, None] == jnp.arange(vocab_local)[None, :]
        row_max = lax.pmax(jnp.max(logits, axis=-1), "tp")
        shifted_exp = jnp.exp(logits - row_max[:, None])
        token_stats = jnp.stack([jnp.sum(shifted_exp, axis=-1), jnp.sum(jnp.where(is_label, logits, 0.0), axis=-1)], axis=0)
        token_stats = lax.psum(token_stats, "tp")
        exp_total = token_stats[0]
        log_norm = row_max + jnp.log(exp_total)
        tok_count = lax.psum(jnp.sum(mask).astype(jnp.float32), "dp")
        weight = mask.reshape(tokens).astype(jnp.float32) / tok_count
        total_loss = lax.psum(jnp.sum(weight * (log_norm - token_stats[1])), "dp")
        soft_probs = shifted_exp * (1.0 / exp_total)[:, None]
        grad_logits = (jnp.where(is_label, soft_probs - 1.0, soft_probs) * weight[:, None]).astype(jnp.bfloat16)
        grad_w = lax.dot_general(unit_rows, grad_logits, (((0,), (0,)), ((), ())), preferred_element_type=jnp.float32)
        grad_w = lax.psum(grad_w, "dp")
        grad_unit = lax.dot_general(grad_logits, w_head, (((1,), (1,)), ((), ())), preferred_element_type=jnp.float32)
        grad_unit = lax.psum(grad_unit, "tp")
        grad_gamma = lax.psum(jnp.sum(grad_unit * normed, axis=0), "dp")
        grad_normed = grad_unit * gamma
        grad_rows = inv_rms * (grad_normed - normed * jnp.mean(grad_normed * normed, axis=-1, keepdims=True))
        grad_hidden = grad_rows.astype(jnp.bfloat16).reshape(num_seqs, seqlen, dmodel)
        return total_loss, grad_hidden, grad_w, grad_gamma

    return jax.shard_map(
        local_step,
        mesh=mesh,
        in_specs=(P("dp", None, None), P(), P(None, "tp"), P("dp", None), P("dp", None)),
        out_specs=(P(), P("dp", None, None), P(None, "tp"), P()),
        check_vma=False,
    )
```

profile of v0, /device:TPU:1, one launch (start us, length us, event | category | flops | bytes accessed | tf_op | source)
XLA Modules:
  0.0 950.9 jit_solution(15515464482360756834)
XLA Ops:
  7.2 0.0 all-reduce.4.cloned.1.call-start
  7.2 1.3 reduce_sum.63
  9.2 13.7 %psum.42 = f32[]{:T(128)} all-reduce(f32[]{:T(128)S(6)} %convert_element_type.30), channel_id=1, replica_groups=mesh['tp'=16,'dp'=8] {'dp'}, use_global_device_ids=true, to_apply=%region_1.0 | all-reduce | flops 1 | bytes 8 | tf_op jit(solution)/shard_map/psum | solution.py:27
  22.9 0.7 subtract_bitcast_fusion
  23.6 1.3 divide_bitcast_fusion
  24.9 2.6 multiply_reduce_fusion.2
  27.5 0.0 copy-start.2
  27.6 0.6 copy-done.2
  28.1 2.7 multiply_convert_fusion.1
  30.8 37.3 %fusion.7 = (f32[1024]{0:T(1024)S(1)}, f32[1024,9496]{0,1:T(8,128)}) fusion(bf16[1024,1536]{1,0:T(8,128)(2,1)S(1)} %multiply_convert_fusion.1, bf16[1536,9496]{0,1:T(8,128)(2,1)} %param.7), kind=kOutput, calls=%fused_computation.23 | convolution fusion | flops 29881556992 | bytes 71217152 | tf_op jit(solution)/shard_map/dot_general | solution.py:18
  68.1 35.1 %pmax.7 = f32[1024]{0:T(1024)S(1)} all-reduce(f32[1024]{0:T(1024)S(1)} %get-tuple-element.13), channel_id=1, replica_groups=mesh['tp'=16,'dp'=8] {'tp'}, use_global_device_ids=true, to_apply=%region_4.5 | all-reduce | flops 1024 | bytes 8192 | tf_op jit(solution)/shard_map/pmax | solution.py:21
  103.2 17.3 %fusion.2 = (f32[1024]{0:T(1024)S(1)}, f32[1024]{0:T(1024)S(1)}) fusion(f32[1024,9496]{0,1:T(8,128)} %get-tuple-element.14, f32[1024]{0:T(1024)S(1)} %pmax.7, s32[1024]{0:T(1024)S(1)} %bitcast.33), kind=kLoop, calls=%fused_computation.6 | loop fusion | flops 48617472 | bytes 38912000 | tf_op jit(solution)/shard_map/reduce_sum | solution.py:23
  120.5 29.2 %psum.43 = f32[2,1024]{1,0:T(2,128)S(1)} all-reduce(f32[2,1024]{1,0:T(2,128)S(1)} %pad_maximum_fusion), channel_id=1, replica_groups=mesh['tp'=16,'dp'=8] {'tp'}, use_global_device_ids=true, to_apply=%region_7.8 | all-reduce | flops 2048 | bytes 16384 | tf_op jit(solution)/shard_map/psum | solution.py:24
  149.8 46.2 %fusion.5 = f32[1024,1536]{1,0:T(8,128)} fusion(bf16[1536,9496]{0,1:T(8,128)(2,1)} %param.7, f32[1024,9496]{0,1:T(8,128)} %get-tuple-element.14, f32[1024]{0:T(1024)S(1)} %bitcast.40, f32[1024]{0:T(1024)S(1)} %bitcast.43, s32[1024]{0:T(1024)S(1)} %bitcast.34, f32[1024]{0:T(1024)S(1)} %pmax.7), kind=kOutput, calls=%fused_computation.22 | convolution fusion | flops 29939900416 | bytes 74375168 | tf_op jit(solution)/shard_map/dot_general | solution.py:34
  195.9 0.0 all-reduce.4.cloned.1.call-update
  196.0 0.3 all-reduce.6.cloned.1.call-start
  196.2 43.8 %fusion.3 = f32[1536,9496]{0,1:T(8,128)} fusion(bf16[1024,1536]{1,0:T(8,128)(2,1)S(1)} %multiply_convert_fusion.1, f32[1024,9496]{0,1:T(8,128)} %get-tuple-element.14, f32[1024]{0:T(1024)S(1)} %bitcast.41, f32[1024]{0:T(1024)S(1)} %bitcast.44, s32[1024]{0:T(1024)S(1)} %bitcast.35, f32[1024]{0:T(1024)S(1)} %pmax.7), kind=kOutput, calls=%fused_computation.21 | convolution fusion | flops 29939900416 | bytes 100401152 | tf_op jit(solution)/shard_map/dot_general | solution.py:32
  240.1 0.0 copy-start
  240.1 0.0 copy-start.1
  240.1 0.0 copy-start.3
  240.1 0.0 all-reduce.6.cloned.1.call-update
  240.1 0.6 multiply_reduce_fusion.3
  240.7 88.6 %all-reduce.4.cloned.1.call-done = f32[1024,1536]{1,0:T(8,128)} async-done(((f32[1024,1536]{1,0:T(8,128)}), f32[1024,1536]{1,0:T(8,128)}) %all-reduce.4.cloned.1.call-update) | async-done | bytes 6291472 | tf_op jit(solution)/shard_map/psum | solution.py:35
  329.3 0.0 copy-done
  329.3 0.0 copy-done.1
  329.3 0.0 copy-done.3
  329.3 4.0 multiply_reduce_fusion
  333.3 13.9 %all-reduce = (f32[]{:T(128)}, f32[1536]{0:T(1024)}) all-reduce(f32[]{:T(128)} %multiply_reduce_fusion.3, f32[1536]{0:T(1024)S(1)} %get-tuple-element.6), channel_id=1, replica_groups=mesh['tp'=16,'dp'=8] {'dp'}, use_global_device_ids=true, to_apply=%region_9.10 | all-reduce | flops 1537 | bytes 12296 | tf_op jit(solution)/shard_map/psum | solution.py:29
  347.3 4.8 multiply_convert_fusion
  352.1 552.9 %all-reduce.6.cloned.1.call-done = f32[1536,9496]{0,1:T(8,128)} async-done(((f32[1536,9496]{0,1:T(8,128)}), f32[1536,9496]{0,1:T(8,128)}) %all-reduce.6.cloned.1.call-update) | async-done | bytes 58343440 | tf_op jit(solution)/shard_map/psum | solution.py:33
  905.0 39.1 %copy.14 = f32[1536,9496]{0,1:T(8,128)} copy(f32[1536,9496]{0,1:T(8,128)} %all-reduce.6.cloned.1.call-done) | data formatting | bytes 116686848
  (7 shorter events, 0.1 us)
Async XLA Ops:
  7.2 322.2 %all-reduce.4.cloned.1.call-start = ((), (), s32[]{:S(2)}) async-start(), calls=%async_computation | async-start | bytes 12582912 | tf_op jit(solution)/shard_map/psum | solution.py:35
  27.5 0.6 copy-start.2
  196.0 709.0 %all-reduce.6.cloned.1.call-start = ((), (), s32[]{:S(2)}) async-start(), calls=%async_computation.1 | async-start | bytes 116686848 | tf_op jit(solution)/shard_map/psum | solution.py:33
  240.1 89.3 %copy-start = (bf16[2,512,1536]{2,1,0:T(8,128)(2,1)S(1)}, bf16[2,512,1536]{2,1,0:T(8,128)(2,1)}, u32[]{:S(2)}) copy-start(bf16[2,512,1536]{2,1,0:T(8,128)(2,1)} %param.5) | copy-start | bytes 9437188
  240.1 89.3 %copy-start.1 = (f32[1536]{0:T(1024)S(1)}, f32[1536]{0:T(1024)}, u32[]{:S(2)}) copy-start(f32[1536]{0:T(1024)} %param.6) | copy-start | bytes 18436
  240.1 89.3 %copy-start.3 = (f32[1,4,2,128]{3,1,2,0:T(4,128)S(1)}, f32[1,4,2,128]{3,1,2,0:T(4,128)}, u32[]{:S(2)}) copy-start(f32[1,4,2,128]{3,1,2,0:T(4,128)} %copy-done.2) | copy-start | bytes 12292
Sparse Core Ops, SparseCore 0:
  196.1 133.1 all-reduce.3
  332.4 572.5 all-reduce.5
where the time goes:
time: 952 us; the launch traced here: 951 us
  waiting for transfers between devices  642 us (67%)
  matrix products  127 us (13%)
  blocking collectives  91.9 us (10%)
  local copies, waits for them, and re-layouts  39.7 us (4%)
  other arithmetic  35.3 us (4%)
  between operations  14.8 us (2%)
    psum x1, waiting for transfers between devices, local_step(): grad_w = lax.psum(grad_w, 'dp')  553 us
    psum x1, waiting for transfers between devices, local_step(): grad_unit = lax.psum(grad_unit, 'tp')  88.6 us
    dot_general x1, matrix products, local_step(): lax.dot_general(grad_logits, w_head, (((1,), (1,)), ((), ())), preferred_...  46.2 us
    dot_general x1, matrix products, local_step(): lax.dot_general(unit_rows, grad_logits, (((0,), (0,)), ((), ())), preferr...  43.8 us
    unnamed x12, local copies, waits for them, and re-layouts  39.7 us
    dot_general x1, matrix products, local_step(): logits = jnp.dot(unit_rows, w_head, preferred_element_type=jnp.float32)  37.3 us
    pmax x1, blocking collectives, local_step(): row_max = lax.pmax(jnp.max(logits, axis=-1), 'tp')  35.1 us
    psum x1, blocking collectives, local_step(): token_stats = lax.psum(token_stats, 'tp')  29.2 us
  transfers between devices with their start and end apart: 2, of which 2 were waited for; matrix products, arithmetic and copies ran while one was open for 6% of the time, Pallas kernels for 0%

commit v1 on v0

v1 whole, which is shorter than its diff:
```python
import functools

import jax
import jax.numpy as jnp
from jax import lax
from jax.experimental import pallas as pl
from jax.experimental.pallas import tpu as pltpu
from jax.sharding import Mesh, PartitionSpec as P

EPS = 1e-5
F32=jnp.float32; BF16=jnp.bfloat16
ANY = pl.BlockSpec(memory_space=pl.ANY)
SMEM = pl.BlockSpec(memory_space=pltpu.SMEM)
VMEM = pl.BlockSpec(memory_space=pltpu.VMEM)
D=1536; VL=9496; GROUP=16; CHUNK=512; PER=CHUNK//GROUP
BIG=1e30
def params(mib, **kw):
    return pltpu.CompilerParams(vmem_limit_bytes=mib * 1024 * 1024, **kw)
def cost(flops, nbytes):
    return pl.CostEstimate(flops=int(flops), bytes_accessed=int(nbytes), transcendentals=0)

def gw_kernel(segs, scal, tbl, winv_ref, sl_ref, u_hbm, w_hbm, out_in, out_ref, *rest):
    del out_in
    n = len(segs)
    sends, (ubuf, wbuf, acc, u_sem, w_sem, o_sem) = rest[:n], rest[n:]
    steps = scal[0]
    offs = [sum(segs[:k]) for k in range(n)]
    rows = [pl.multiple_of(scal[1 + k], 8) for k in range(n)]

    def fetch(i, slot):
        for g in range(PER):
            src = pl.multiple_of(tbl[i * PER + g], GROUP)
            pltpu.make_async_copy(u_hbm.at[pl.ds(src, GROUP), :], ubuf.at[slot, pl.ds(g * GROUP, GROUP), :], u_sem.at[slot]).start()

    cps = []
    for k, size in enumerate(segs):
        cps.append(pltpu.make_async_copy(w_hbm.at[pl.ds(rows[k], size), :], wbuf.at[pl.ds(offs[k], size), :], w_sem.at[k]))
    for cp in cps:
        cp.start()
    fetch(0, 0)
    acc[...] = jnp.zeros_like(acc)
    for cp in cps:
        cp.wait()
    winv = winv_ref[0]

    def body(i, _):
        slot = lax.rem(i, 2)
        pltpu.make_async_copy(u_hbm.at[pl.ds(0, CHUNK), :], ubuf.at[slot], u_sem.at[slot]).wait()
        fetch(jnp.minimum(i + 1, steps - 1), 1 - slot)
        u = ubuf[slot].astype(BF16)
        z = lax.dot_general(wbuf[...], u, (((1,), (1,)), ((), ())), preferred_element_type=F32)
        shift = sl_ref[0, pl.ds(i, 1), :]
        lab = sl_ref[1, pl.ds(i, 1), :]
        gs = []
        for k, size in enumerate(segs):
            ids = lax.broadcasted_iota(jnp.int32, (size, CHUNK), 0).astype(F32)
            rel = lab - rows[k].astype(F32)
            gs.append((jnp.exp(z[offs[k]:offs[k] + size] - shift) - jnp.where(ids == rel, winv, 0.0)).astype(BF16))
        g = jnp.concatenate(gs, axis=0) if n > 1 else gs[0]
        acc[...] += jnp.dot(g, u, preferred_element_type=F32)
        return 0

    lax.fori_loop(0, steps, body, 0)
    pltpu.make_async_copy(u_hbm.at[pl.ds(0, CHUNK), :], ubuf.at[0], u_sem.at[lax.rem(steps, 2)]).wait()
    cps = []
    for k, size in enumerate(segs):
        src = acc.at[pl.ds(offs[k], size), :]
        cps.append(pltpu.make_async_copy(src, sends[k], o_sem.at[2 * k]))
        cps.append(pltpu.make_async_copy(src, out_ref.at[pl.ds(rows[k], size), :], o_sem.at[2 * k + 1]))
    for cp in cps:
        cp.start()
    for cp in cps:
        cp.wait()

def gw_call(segs, scal, tbl, winv, sl, u, w, out):
    n = len(segs)
    width = sum(segs)
    dma = pltpu.SemaphoreType.DMA
    res = pl.pallas_call(
        functools.partial(gw_kernel, segs),
        in_specs=[SMEM, SMEM, SMEM, VMEM] + [ANY] * 3,
        out_specs=[ANY] * (n + 1),
        out_shape=[jax.ShapeDtypeStruct((VL, D), F32)] + [jax.ShapeDtypeStruct((s, D), F32) for s in segs],
        scratch_shapes=[
            pltpu.VMEM((2, CHUNK, D), F32),
            pltpu.VMEM((width, D), BF16), pltpu.VMEM((width, D), F32),
            dma((2,)), dma((n,)), dma((2 * n,)),
        ],
        input_output_aliases={6: 0},
        compiler_params=params(48),
        cost_estimate=cost(2 * 2 * 5000 * D * width, 40e6),
        name="grad_w_" + str(width),
    )(scal, tbl, winv, sl, u, w, out)
    return res[0], res[1:]

MESH = pl.DeviceIdType.MESH
VB=512; NFULL=VL//VB; TAIL=VL-NFULL*VB
ROWS=1024


def own_kernel(uf, ub_ref, w_hbm, meta_ref, u_out, du_out, sl_ref, meta_out, misc_ref,
               z_ref, wbuf, du, m_ref, s_ref, l_ref, st_buf, st_mine, lz_buf,
               ssem, rsem, s_send, s_recv, m_send, m_recv, l_send, l_recv, w_sem, c_sem):
    zi, yi, xi, ci = (lax.axis_index(n) for n in ("z", "y", "x", "c"))
    tp = zi * 4 + yi
    rank = xi * 2 + ci
    up = lambda i: lax.rem(i + 1, 4)
    dn = lambda i: lax.rem(i + 3, 4)
    op = lambda i: lax.rem(i + 2, 4)
    xp, xm, x2 = up(xi), dn(xi), op(xi)
    yp, ym, y2 = up(yi), dn(yi), op(yi)
    zp, zm, z2 = up(zi), dn(zi), op(zi)
    plane = [lax.rem(tp + k, 16) for k in range(1, 16)]
    line = [lax.rem(rank + k, 8) for k in range(1, 8)]
    pid = lambda q: {"z": q // 4, "y": lax.rem(q, 4)}
    lid = lambda q: {"x": q // 2, "c": lax.rem(q, 2)}

    def remote(src, dst, ssem_, rsem_, dev):
        return pltpu.make_async_remote_copy(src_ref=src, dst_ref=dst, send_sem=ssem_, recv_sem=rsem_, device_id=dev, device_id_type=MESH)

    lo, hi, al = pl.ds(0, 32), pl.ds(32, 32), pl.ds(0, 4)

    def regions(c):
        rm, rp, r2 = 2 * xm + c, 2 * xp + c, 2 * x2 + c
        a0 = lambda z, y: u_out.at[rm, z, y, lo]
        b0 = lambda z, y: u_out.at[r2, z, y, lo]
        a1 = lambda z, y: u_out.at[rp, z, y, lo]
        b1 = lambda z, y: u_out.at[r2, z, y, hi]
        return dict(
            a0=a0, b0=b0, a1=a1, b1=b1,
            a0row=lambda z: u_out.at[rm, z, al, lo], b0row=lambda z: u_out.at[r2, z, al, lo],
            a1col=lambda y: u_out.at[rp, al, y, lo], b1col=lambda y: u_out.at[r2, al, y, hi],
            xdm=u_out.at[rm, al, al, hi], xdp=u_out.at[rp, al, al, hi], x2=u_out.at[r2, zi, yi],
        )

    R = regions(ci)
    X_P, X_M, X_2 = {"x": xp}, {"x": xm}, {"x": x2}
    Y_P, Y_M, Z_P, Z_M, PAL = {"y": yp}, {"y": ym}, {"z": zp}, {"z": zm}, {"c": 1 - ci}
    msgs = {}

    def add(k, src, dev, arrives, dst=None):
        msgs[k] = (src, src if dst is None else dst, dev, arrives)

    mine = uf.at[zi, yi]
    add(0, uf.at[zi, yi, lo], X_P, R["a0"](zi, yi), u_out.at[rank, zi, yi, lo])
    add(1, uf.at[zi, yi, lo], X_M, R["a1"](zi, yi), u_out.at[rank, zi, yi, lo])
    add(2, mine, X_2, R["x2"], u_out.at[rank, zi, yi])
    add(3, uf.at[al, al, hi], X_P, R["xdm"], u_out.at[rank, al, al, hi])
    add(4, uf.at[al, al, hi], X_M, R["xdp"], u_out.at[rank, al, al, hi])
    add(5, R["a0"](zi, yi), Y_P, R["a0"](zi, ym))
    add(6, R["a0"](zi, yi), Y_M, R["a0"](zi, yp))
    add(7, R["b0"](zi, yi), Y_P, R["b0"](zi, ym))
    add(8, R["b0"](zi, yi), Y_M, R["b0"](zi, yp))
    add(9, R["a0"](zi, ym), Y_P, R["a0"](zi, y2))
    add(10, R["b0"](zi, yp), Y_M, R["b0"](zi, y2))
    add(11, R["a0row"](zi), Z_P, R["a0row"](zm))
    add(12, R["a0row"](zi), Z_M, R["a0row"](zp))
    add(13, R["b0row"](zi), Z_P, R["b0row"](zm))
    add(14, R["b0row"](zi), Z_M, R["b0row"](zp))
    add(15, R["a0row"](zm), Z_P, R["a0row"](z2))
    add(16, R["b0row"](zp), Z_M, R["b0row"](z2))
    add(17, R["a1"](zi, yi), Z_P, R["a1"](zm, yi))
    add(18, R["a1"](zi, yi), Z_M, R["a1"](zp, yi))
    add(19, R["b1"](zi, yi), Z_P, R["b1"](zm, yi))
    add(20, R["b1"](zi, yi), Z_M, R["b1"](zp, yi))
    add(21, R["a1"](zm, yi), Z_P, R["a1"](z2, yi))
    add(22, R["b1"](zp, yi), Z_M, R["b1"](z2, yi))
    add(23, R["a1col"](yi), Y_P, R["a1col"](ym))
    add(24, R["a1col"](yi), Y_M, R["a1col"](yp))
    add(25, R["b1col"](yi), Y_P, R["b1col"](ym))
    add(26, R["b1col"](yi), Y_M, R["b1col"](yp))
    add(27, R["a1col"](ym), Y_P, R["a1col"](y2))
    add(28, R["b1col"](yp), Y_M, R["b1col"](y2))
    Q = regions(1 - ci)
    add(29, uf, PAL, u_out.at[2 * xi + 1 - ci], u_out.at[rank])
    add(30, R["xdm"], PAL, Q["xdm"])
    add(31, R["xdp"], PAL, Q["xdp"])
    for k, (n, i) in enumerate([("a0row", zi), ("b0row", zi), ("a0row", zm), ("a0row", zp), ("a0row", z2), ("b0row", zm), ("b0row", zp), ("b0row", z2),
                                ("a1col", yi), ("b1col", yi), ("a1col", ym), ("a1col", yp), ("a1col", y2), ("b1col", ym), ("b1col", yp), ("b1col", y2)]):
        add(32 + k, R[n](i), PAL, Q[n](i))

    def send(*ks):
        for k in ks:
            src, dst, dev, _ = msgs[k]
            remote(src, dst, ssem.at[k], rsem.at[k], dev).start()

    def got(*ks):
        for k in ks:
            _, _, dev, reg = msgs[k]
            remote(reg, reg, ssem.at[k], rsem.at[k], dev).wait_recv()

    def sent(*ks):
        for k in ks:
            src, dst, dev, _ = msgs[k]
            remote(src, dst, ssem.at[k], rsem.at[k], dev).wait_send()

    bar = pltpu.get_barrier_semaphore()
    for q in plane:
        pl.semaphore_signal(bar, inc=1, device_id=pid(q), device_id_type=MESH)
    for q in line:
        pl.semaphore_signal(bar, inc=1, device_id=lid(q), device_id_type=MESH)
    pl.semaphore_wait(bar, 22)

    def w_copy(j, slot, size=VB):
        return pltpu.make_async_copy(w_hbm.at[pl.ds(pl.multiple_of(j * VB, VB), size), :], wbuf.at[slot, pl.ds(0, size)], w_sem.at[slot])

    w_copy(0, 0).start()
    line_msgs = []
    for k, q in enumerate(line):
        cp = remote(meta_ref, meta_out.at[rank], m_send.at[k], m_recv.at[rank], lid(q))
        cp.start()
        line_msgs.append(cp)
    send(0, 1, 2, 3, 4, 29)
    stage = [(uf.at[t // 4, t % 4], du.at[pl.ds(64 * t, 64)], u_out.at[rank, t // 4, t % 4]) for t in range(16)]
    for a, b, _ in stage:
        pltpu.make_async_copy(a, b, c_sem.at[0]).start()
    meta_out[rank] = meta_ref[...]
    m_ref[...] = jnp.full_like(m_ref, -BIG)
    s_ref[...] = jnp.zeros_like(s_ref)
    l_ref[...] = jnp.zeros_like(l_ref)

    def as_row(v):
        return jnp.concatenate([v[i:i + 1, :] for i in range(8)], axis=1)

    lab = as_row((meta_ref[0] - tp * VL).astype(F32))

    def stats(j, slot, size):
        z = lax.dot_general(wbuf[slot, :size], ub_ref[...], (((1,), (1,)), ((), ())), preferred_element_type=F32)
        z_ref[pl.ds(pl.multiple_of(j * VB, VB), size), :] = z
        zz = z.reshape(size // 8, 8, ROWS)
        ids = lax.broadcasted_iota(jnp.int32, (size, ROWS), 0).astype(F32)
        rel = lab - (j * VB) * 1.0
        m_old = m_ref[...]
        m_new = jnp.maximum(m_old, jnp.max(zz, axis=0))
        s_ref[...] = s_ref[...] * jnp.exp(m_old - m_new) + jnp.sum(jnp.exp(zz - m_new[None]), axis=0)
        l_ref[...] += jnp.sum(jnp.where(ids == rel, z, 0.0).reshape(size // 8, 8, ROWS), axis=0)
        m_ref[...] = m_new

    def at(j, k, fn):
        @pl.when(j == k)
        def _():
            fn()

    def copy_out():
        for a, b, _ in stage:
            pltpu.make_async_copy(a, b, c_sem.at[0]).wait()
        for _, b, c in stage:
            pltpu.make_async_copy(b, c, c_sem.at[1]).start()

    def first_a():
        got(0, 1)
        send(5, 6, 17, 18)

    def first_b():
        got(2)
        send(7, 8, 19, 20)

    def hop_a():
        got(5, 17)
        send(9, 21)

    def hop_b():
        got(8, 20)
        send(10, 22)

    def stream(j):
        slot = lax.rem(j, 2)
        w_copy(j, slot).wait()

        @pl.when(j < NFULL - 1)
        def _():
            w_copy(j + 1, 1 - slot).start()

        @pl.when(j == NFULL - 1)
        def _():
            w_copy(NFULL, 1 - slot, TAIL).start()

        return slot

    def stats_step(j, _):
        slot = stream(j)
        stats(j, slot, VB)
        at(j, 2, copy_out)
        at(j, 4, first_a)
        at(j, 8, hop_a)
        at(j, 9, first_b)
        at(j, 13, hop_b)
        return 0

    lax.fori_loop(0, NFULL, stats_step, 0)
    w_copy(NFULL, NFULL % 2, TAIL).wait()
    stats(NFULL, NFULL % 2, TAIL)
    w_copy(0, 0).start()
    for _, b, c in stage:
        pltpu.make_async_copy(b, c, c_sem.at[1]).wait()

    m8 = m_ref[...]
    top = jnp.max(m8, axis=0, keepdims=True)
    tot = jnp.sum(s_ref[...] * jnp.exp(m8 - top), axis=0, keepdims=True)
    hit = jnp.sum(l_ref[...], axis=0, keepdims=True)

    def as_tile(v):
        return jnp.concatenate([v[:, 128 * i:128 * i + 128] for i in range(8)], axis=0)

    for k, v in enumerate((top, tot, hit)):
        st_mine[k] = as_tile(v)
        st_buf[tp, k] = as_tile(v)
    plane_msgs = []
    for k, q in enumerate(plane):
        cp = remote(st_mine, st_buf.at[tp], s_send.at[k], s_recv.at[tp], pid(q))
        cp.start()
        plane_msgs.append(cp)
    got(6, 9)
    send(11, 12, 32)
    got(18, 21)
    send(23, 24, 40)
    got(7, 10)
    send(13, 14, 33)
    got(19, 22)
    send(25, 26, 41)
    for k, q in enumerate(line):
        remote(meta_ref, meta_out.at[q], m_send.at[k], m_recv.at[q], lid(q)).wait_recv()
    count = jnp.zeros((8, 128), F32)
    for r in range(8):
        count += meta_out[r, 1].astype(F32)
    count = jnp.broadcast_to(jnp.sum(jnp.sum(count, axis=1, keepdims=True), axis=0, keepdims=True), (8, 128))
    log_n = jnp.log(count)
    for k, q in enumerate(plane):
        remote(st_mine, st_buf.at[q], s_send.at[k], s_recv.at[q], pid(q)).wait_recv()
    top = st_buf[0, 0]
    for q in range(1, 16):
        top = jnp.maximum(top, st_buf[q, 0])
    total = jnp.zeros_like(top)
    label = jnp.zeros_like(top)
    for q in range(16):
        total += st_buf[q, 1] * jnp.exp(st_buf[q, 0] - top)
        label += st_buf[q, 2]
    lse = top + jnp.log(total)
    lz_buf[rank, 0] = lse
    lz_buf[rank, 1] = label
    on = meta_ref[1] > 0
    shift = as_row(jnp.where(on, lse + log_n, BIG))
    lab_on = as_row(jnp.where(on, (meta_ref[0] - tp * VL).astype(F32), -BIG))
    winv = as_row(1.0 / count)
    for k, q in enumerate(line):
        cp = remote(lz_buf.at[rank], lz_buf.at[rank], l_send.at[k], l_recv.at[rank], lid(q))
        cp.start()
        line_msgs.append(cp)

    du[...] = jnp.zeros_like(du)

    def grad(j, slot, size):
        z = z_ref[pl.ds(pl.multiple_of(j * VB, VB), size), :]
        ids = lax.broadcasted_iota(jnp.int32, (size, ROWS), 0).astype(F32)
        rel = lab_on - (j * VB) * 1.0
        g = (jnp.exp(z - shift) - jnp.where(ids == rel, winv, 0.0)).astype(BF16)
        du[...] += lax.dot_general(g, wbuf[slot, :size], (((0,), (0,)), ((), ())), preferred_element_type=F32)

    def arrive_a():
        got(11)
        send(15, 34)
        got(23)
        send(27, 42)
        got(12)
        send(35)
        got(24)
        send(43)

    def arrive_b():
        got(14)
        send(16, 38)
        got(26)
        send(28, 46)
        got(13)
        send(37)
        got(25)
        send(45)

    def arrive_x():
        got(3)
        send(30)
        got(4)
        send(31)

    def grad_step(j, _):
        slot = stream(j)
        grad(j, slot, VB)
        at(j, 5, arrive_a)
        at(j, 13, arrive_b)
        at(j, 16, arrive_x)
        return 0

    lax.fori_loop(0, NFULL, grad_step, 0)
    w_copy(NFULL, NFULL % 2, TAIL).wait()
    grad(NFULL, NFULL % 2, TAIL)
    out = pltpu.make_async_copy(du, du_out, c_sem.at[0])
    out.start()

    for k, q in enumerate(line):
        remote(lz_buf.at[q], lz_buf.at[q], l_send.at[k], l_recv.at[q], lid(q)).wait_recv()
    loss = jnp.zeros((8, 128), F32)
    for r in range(8):
        on = meta_out[r, 1] > 0
        lse = lz_buf[r, 0]
        loss += jnp.where(on, (lse - lz_buf[r, 1]) / count, 0.0)
        sl_ref[0, r] = jnp.where(on, lse + log_n, BIG)
        sl_ref[1, r] = jnp.where(on, (meta_out[r, 0] - tp * VL).astype(F32), -BIG)
    loss = jnp.sum(jnp.sum(loss, axis=1, keepdims=True), axis=0, keepdims=True)
    sub = lax.broadcasted_iota(jnp.int32, (8, 128), 0)
    misc_ref[...] = jnp.where(sub == 0, jnp.broadcast_to(loss, (8, 128)), 1.0 / count)
    got(15)
    send(36)
    got(27)
    send(44)
    got(16)
    send(39)
    got(28)
    send(47)
    for k in range(29, 48):
        got(k)
    for cp in line_msgs + plane_msgs:
        cp.wait_send()
    sent(*range(48))
    out.wait()


def own_call(uf, ub, wt, meta):
    dma = pltpu.SemaphoreType.DMA
    return pl.pallas_call(
        own_kernel,
        in_specs=[ANY, VMEM, ANY, VMEM],
        out_specs=[ANY, ANY, VMEM, VMEM, VMEM],
        out_shape=[
            jax.ShapeDtypeStruct((8, 4, 4, 64, D), F32),
            jax.ShapeDtypeStruct((ROWS, D), F32),
            jax.ShapeDtypeStruct((2, 8, 8, 128), F32),
            jax.ShapeDtypeStruct((8, 2, 8, 128), jnp.int32),
            jax.ShapeDtypeStruct((8, 128), F32),
        ],
        scratch_shapes=[
            pltpu.VMEM((VL, ROWS), F32), pltpu.VMEM((2, VB, D), BF16), pltpu.VMEM((ROWS, D), F32),
            pltpu.VMEM((8, ROWS), F32), pltpu.VMEM((8, ROWS), F32), pltpu.VMEM((8, ROWS), F32),
            pltpu.VMEM((16, 3, 8, 128), F32), pltpu.VMEM((3, 8, 128), F32), pltpu.VMEM((8, 2, 8, 128), F32),
            dma((48,)), dma((48,)), dma((15,)), dma((16,)), dma((7,)), dma((8,)), dma((7,)), dma((8,)), dma((2,)), dma((2,)),
        ],
        compiler_params=params(62, collective_id=0, has_side_effects=True),
        cost_estimate=cost(4 * ROWS * D * VL, 200e6),
        name="own_rank",
    )(uf, ub, wt, meta)

SEG = 384
S_ROWS = 1536


def place_kernel(nsrc, rows, depth, where, *refs):
    srcs, out_ref, (buf, in_sem, out_sem) = refs[:nsrc], refs[nsrc + 1], refs[nsrc + 2:]
    jobs = []
    for k in range(nsrc):
        n = srcs[k].shape[0]
        for r in range(0, n, rows):
            jobs.append((k, r, min(rows, n - r)))

    def load(q):
        k, r, size = jobs[q]
        return pltpu.make_async_copy(srcs[k].at[pl.ds(r, size), :], buf.at[q % depth, pl.ds(0, size), :], in_sem.at[q % depth])

    def store(q):
        k, r, size = jobs[q]
        dst = out_ref.at[pl.ds(pl.multiple_of(where[k], 8) + r, size), :]
        return pltpu.make_async_copy(buf.at[q % depth, pl.ds(0, size), :], dst, out_sem.at[q % depth])

    lead = depth // 2
    for q in range(len(jobs) + lead):
        if q < len(jobs):
            if q >= depth:
                store(q - depth).wait()
            load(q).start()
        if q >= lead:
            load(q - lead).wait()
            store(q - lead).start()
    for q in range(max(0, len(jobs) - depth), len(jobs)):
        store(q).wait()


def place_call(where, srcs, out):
    rows, depth, n = 384, 8, len(srcs)
    dma = pltpu.SemaphoreType.DMA
    return pl.pallas_call(
        functools.partial(place_kernel, n, rows, depth),
        in_specs=[SMEM] + [ANY] * (n + 1),
        out_specs=ANY,
        out_shape=jax.ShapeDtypeStruct((VL, D), F32),
        scratch_shapes=[pltpu.VMEM((depth, rows, D), F32), dma((depth,)), dma((depth,))],
        input_output_aliases={n + 1: 0},
        compiler_params=params(32),
        cost_estimate=cost(1e10, 80e6),
        name="place_" + str(n),
    )(where, *srcs, out)


def alloc_kernel(x_ref, o_ref):
    del x_ref, o_ref


def alloc_out(dep):
    return pl.pallas_call(
        alloc_kernel, in_specs=[ANY], out_specs=ANY, out_shape=jax.ShapeDtypeStruct((VL, D), F32), name="alloc",
    )(dep)


def local_step(hidden, gamma, w, labels, mask):
    num_seqs, seqlen, _ = hidden.shape
    tokens = num_seqs * seqlen
    zi, yi, xi, ci = (lax.axis_index(n) for n in ("z", "y", "x", "c"))
    swap = [(0, 1), (1, 0)]
    wt = w.T

    rows = hidden.reshape(tokens, D).astype(F32)
    inv = lax.rsqrt(jnp.mean(rows * rows, axis=-1, keepdims=True) + EPS)
    u = (rows * inv * gamma).astype(BF16)
    meta = jnp.stack([labels.reshape(8, 128), mask.reshape(8, 128)])
    u_all, du, sl, meta_all, misc = own_call(u.astype(F32).reshape(4, 4, 64, D), u, wt, meta)
    u_all = u_all.reshape(8192, D)
    loss = misc[0, 0]
    winv = misc[1, 0].reshape(1)

    seq_len = meta_all[:, 1].reshape(16, 512).sum(-1)
    groups = (seq_len + GROUP - 1) // GROUP
    pos = jnp.arange(512)
    ids = jnp.arange(16)
    before = jnp.sum(jnp.where(ids[None, :] < ids[:, None], groups[None, :], 0), axis=1)
    total = jnp.sum(groups)
    seq = jnp.sum(pos[:, None] >= (before + groups)[None, :], axis=1)
    start = jnp.sum(jnp.where(ids[None, :] == seq[:, None], before[None, :], 0), axis=1)
    live = pos < total
    grp = jnp.where(live, seq * 32 + pos - start, 0)
    tbl = (grp * GROUP).astype(jnp.int32)
    steps = ((total + PER - 1) // PER).astype(jnp.int32)
    dead = jnp.stack([jnp.full((GROUP,), BIG, F32), jnp.full((GROUP,), -BIG, F32)])[:, None, :]
    slc = jnp.where(live[None, :, None], jnp.take(sl.reshape(2, 512, GROUP), grp, axis=1), dead).reshape(2, 16, CHUNK)

    half = 4752
    base = ci * half
    other = (1 - ci) * half
    even = xi % 2 == 0
    s_off = jnp.where(even, S_ROWS, 0)
    r_off = jnp.where(even, 0, S_ROWS)
    left = [(i, (i + 3) % 4) for i in range(4)]
    right = [(i, (i + 1) % 4) for i in range(4)]
    out = alloc_out(misc)
    pieces, where, hop = [], [], []
    sc = lambda *v: jnp.stack([steps, *v]).astype(jnp.int32)
    for k in range(2):
        offs = [SEG * k, S_ROWS // 2 + SEG * k]
        out, (sl_, sr_) = gw_call((SEG, SEG), sc(*[base + s_off + o for o in offs]), tbl, winv, slc, u_all, wt, out)
        rl = lax.ppermute(sl_, "x", left)
        rr = lax.ppermute(sr_, "x", right)
        for arr, o in ((rl, offs[0]), (rr, offs[1])):
            pieces.append(arr)
            where.append(base + r_off + o)
            hop.append((arr, other + r_off + o))
        for arr, o in ((sl_, offs[0]), (sr_, offs[1])):
            pieces.append(lax.ppermute(arr, "c", swap))
            where.append(other + s_off + o)
    c_off = 2 * S_ROWS
    for o, size in ((c_off, 840), (c_off + 840, 840)):
        lim = VL - size
        out, (cc,) = gw_call((size,), sc(jnp.minimum(base + o, lim)), tbl, winv, slc, u_all, wt, out)
        pieces.append(lax.ppermute(cc, "c", swap))
        where.append(jnp.minimum(other + o, lim))
    for arr, o in hop:
        pieces.append(lax.ppermute(arr, "c", swap))
        where.append(o)
    grad_w = place_call(jnp.stack(where).astype(jnp.int32), pieces, out).T

    du = lax.psum(du, ("z", "y"))
    n = rows * inv
    v = du * gamma
    grad_rows = inv * (v - n * jnp.mean(v * n, axis=-1, keepdims=True))
    grad_hidden = grad_rows.astype(BF16).reshape(num_seqs, seqlen, D)
    gg = jnp.sum(du * n, axis=0, keepdims=True)
    parts = [gg] + [lax.ppermute(gg, "x", [(i, (i + k) % 4) for i in range(4)]) for k in range(1, 4)]
    stack = jnp.concatenate(parts, axis=0)
    order = (xi - jnp.arange(4)) % 4
    gg = sum(jnp.take(stack, order[i:i + 1], axis=0) for i in range(4))
    grad_gamma = (gg + lax.ppermute(gg, "c", swap)).reshape(D)
    return loss, grad_hidden, grad_w, grad_gamma


def solution(mesh):
    fine = Mesh(mesh.devices.reshape(4, 4, 4, 2), ("z", "y", "x", "c"))
    return jax.shard_map(
        local_step,
        mesh=fine,
        in_specs=(P(("x", "c"), None, None), P(), P(None, ("z", "y")), P(("x", "c"), None), P(("x", "c"), None)),
        out_specs=(P(), P(("x", "c"), None, None), P(None, ("z", "y")), P()),
        check_vma=False,
    )
```

time: 952 us -> 397 us (0.42)
  waiting for transfers between devices: 642 us -> 33.5 us
  Pallas kernels: 0 us -> 282 us
  matrix products: 127 us -> 0 us
  blocking collectives: 91.9 us -> 0 us
  local copies, waits for them, and re-layouts: 39.7 us -> 18.2 us
  starting transfers between devices: 0.3 us -> 16.2 us
  other arithmetic: 35.3 us -> 23.8 us
    psum x2 -> x1, waiting for transfers between devices: 642 us -> 0.02 us  [local_step(): du = lax.psum(du, ('z', 'y'))]
    pallas_call x0 -> x7, Pallas kernels: none -> 282 us  [the longest x4 139 us: gw_call(): pl.pallas_call(functools.partial(gw_kernel, segs), in_specs=[SMEM, SMEM,...]
    dot_general x3 -> x0, matrix products: 127 us -> none  [the longest x1 46.2 us: local_step(): lax.dot_general(grad_logits, w_head, (((1,), (1,)), ((), ())), preferred_...]
    psum x3 -> x0, blocking collectives: 56.8 us -> none  [the longest x1 29.2 us: local_step(): token_stats = lax.psum(token_stats, 'tp')]
    pmax x1 -> x0, blocking collectives: 35.1 us -> none  [local_step(): row_max = lax.pmax(jnp.max(logits, axis=-1), 'tp')]
    ppermute x0 -> x18, waiting for transfers between devices: none -> 33.4 us  [the longest x2 24.8 us: local_step(): rl = lax.ppermute(sl_, 'x', left)]
    unnamed x12 -> x37, local copies, waits for them, and re-layouts: 39.7 us -> 10.6 us
    ppermute x0 -> x18, starting transfers between devices: none -> 16.2 us  [the longest x8 5.04 us: local_step(): pieces.append(lax.ppermute(arr, 'c', swap))]
  transfers between devices with their start and end apart: 2 -> 19, of which waited for: 2 -> 8; matrix products, arithmetic and copies ran while one was open for 6% -> 1% of each run, Pallas kernels for 0% -> 25%
where the time goes in v1:
time: 397 us
  Pallas kernels  282 us (71%)
  waiting for transfers between devices  33.5 us (8%)
  other arithmetic  23.8 us (6%)
  between operations  22.8 us (6%)
  local copies, waits for them, and re-layouts  18.2 us (5%)
  starting transfers between devices  16.2 us (4%)
    pallas_call x4, Pallas kernels, gw_call(): pl.pallas_call(functools.partial(gw_kernel, segs), in_specs=[SMEM, SMEM,...  139 us
    pallas_call x1, Pallas kernels, own_call(): pl.pallas_call(own_kernel, in_specs=[ANY, VMEM, ANY, VMEM], out_specs=[AN...  118 us
    pallas_call x1, Pallas kernels, place_call(): pl.pallas_call(functools.partial(place_kernel, n, rows, depth), in_specs=...  24.9 us
    ppermute x2, waiting for transfers between devices, local_step(): rl = lax.ppermute(sl_, 'x', left)  24.8 us
    unnamed x37, local copies, waits for them, and re-layouts  10.6 us
  transfers between devices with their start and end apart: 19, of which 8 were waited for; matrix products, arithmetic and copies ran while one was open for 1% of the time, Pallas kernels for 25%

profile of v1, /device:TPU:1, one launch (start us, length us, event | category | flops | bytes accessed | tf_op | source)
XLA Modules:
  0.0 396.7 jit_solution(3207117138468892199)
XLA Ops:
  7.2 2.7 multiply_reduce_fusion.2
  10.1 0.7 stack_reshape.6
  10.8 0.7 stack_reshape.7
  11.5 4.3 %multiply_convert_fusion.1.ub_ref = bf16[1024,1536]{1,0:T(8,128)(2,1)} fusion(bf16[2,512,1536]{2,1,0:T(8,128)(2,1)} %param.7, f32[1536]{0:T(1024)} %param.8, f32[1024]{0:T(1024)S(1)} %bitcast.69), kind=kLoop, calls=%fused_computation.5 | loop fusion | flops 6291456 | bytes 6301696 | tf_op jit(solution)/shard_map/convert_element_type | solution.py:520
  15.8 3.4 fusion.uf
  19.2 0.6 pad_add_fusion.meta_ref
  19.8 118.2 %own_rank.1 = (f32[8,4,4,64,1536]{4,3,2,1,0:T(8,128)}, f32[1024,1536]{1,0:T(8,128)}, f32[2,8,8,128]{3,2,1,0:T(8,128)}, s32[8,2,8,128]{3,2,1,0:T(8,128)}, f32[8,128]{1,0:T(8,128)}) custom-call(f32[4,4,64,1536]{3,2,1,0:T(8,128)} %fusion.uf, bf16[1024,1536]{1,0:T(8,128)(2,1)} %multiply_convert_fusion.1.ub_ref, bf16[9496,1536]{1,0:T(8,128)(2,1)} %bitcast.61, ...), custom_call_target="tpu_custom_call" | custom-call | flops 59743666176 | bytes 200000000 | tf_op jit(solution)/shard_map/own_rank/pallas_call | solution.py:429
  138.0 1.0 slice_reduce_fusion
  139.1 0.1 reduce_sum.87
  139.2 0.7 fusion.7
  139.8 0.1 select_reduce_fusion.1
  140.2 0.7 broadcast_multiply_fusion.1
  141.6 1.3 fusion.8
  142.9 0.7 compare_select_fusion.1
  143.7 0.2 reshape.173
  143.8 0.4 copy.16
  144.3 2.1 gather_fusion
  146.4 0.3 gather.10
  146.7 0.7 fusion.1
  147.3 0.1 broadcast_in_dim.102
  147.5 0.2 broadcast_in_dim.103
  147.7 0.1 broadcast_in_dim.98
  147.8 0.2 broadcast_in_dim.99
  148.0 0.3 broadcast_in_dim.108
  148.5 32.5 %grad_w_768.2 = (f32[9496,1536]{1,0:T(8,128)}, f32[384,1536]{1,0:T(8,128)S(1)}, f32[384,1536]{1,0:T(8,128)S(1)}) custom-call(s32[3]{0:T(128)S(1)} %get-tuple-element.60.scal, s32[512]{0:T(512)S(1)} %get-tuple-element.55.tbl, f32[1]{0:T(128)} %bitcast.22.winv_ref, f32[2,16,512]{2,1,0:T(8,128)S(1)} %select_select_fusion.sl_ref, ...), custom_call_target="tpu_custom_call", output_to_operand_aliasing={{0}: (6, {})} | custom-call | flops 23592960000 | bytes 40000000 | tf_op jit(solution)/shard_map/grad_w_768/pallas_call | solution.py:79
  181.0 1.4 copy-done.4
  182.4 1.4 copy-done.6
  183.8 33.6 %grad_w_768.3 = (f32[9496,1536]{1,0:T(8,128)}, f32[384,1536]{1,0:T(8,128)}, f32[384,1536]{1,0:T(8,128)}) custom-call(s32[3]{0:T(128)S(1)} %get-tuple-element.61.scal, s32[512]{0:T(512)S(1)} %get-tuple-element.55.tbl, f32[1]{0:T(128)} %bitcast.22.winv_ref, f32[2,16,512]{2,1,0:T(8,128)S(1)} %select_select_fusion.sl_ref, ...), custom_call_target="tpu_custom_call", output_to_operand_aliasing={{0}: (6, {})} | custom-call | flops 23592960000 | bytes 40000000 | tf_op jit(solution)/shard_map/grad_w_768/pallas_call | solution.py:79
  217.6 0.1 collective-permute-start.6
  217.7 1.7 collective-permute-start.5
  219.4 0.4 collective-permute-start.7
  219.8 1.4 collective-permute-start
  221.3 36.4 %grad_w_840.2 = (f32[9496,1536]{1,0:T(8,128)}, f32[840,1536]{1,0:T(8,128)}) custom-call(s32[2]{0:T(128)S(1)} %get-tuple-element.62.scal, s32[512]{0:T(512)S(1)} %get-tuple-element.55.tbl, f32[1]{0:T(128)} %bitcast.22.winv_ref, f32[2,16,512]{2,1,0:T(8,128)S(1)} %select_select_fusion.sl_ref, f32[8192,1536]{1,0:T(8,128)} %bitcast.59, ...), custom_call_target="tpu_custom_call", output_to_operand_aliasing={{0}: (6, {})} | custom-call | flops 25804800000 | bytes 40000000 | tf_op jit(solution)/shard_map/grad_w_840/pallas_call | solution.py:79
  257.7 12.7 %collective-permute-done.4.refs_4_ = f32[384,1536]{1,0:T(8,128)S(1)} collective-permute-done((f32[384,1536]{1,0:T(8,128)}, f32[384,1536]{1,0:T(8,128)S(1)}, u32[]{:S(2)}, u32[]{:S(2)}) %collective-permute-start.4) | collective-permute-done | bytes 2359328 | tf_op jit(solution)/shard_map/ppermute | solution.py:556
  270.4 36.4 %grad_w_840.3 = (f32[9496,1536]{1,0:T(8,128)}, f32[840,1536]{1,0:T(8,128)}) custom-call(s32[2]{0:T(128)S(1)} %get-tuple-element.63.scal, s32[512]{0:T(512)S(1)} %get-tuple-element.55.tbl, f32[1]{0:T(128)} %bitcast.22.winv_ref, f32[2,16,512]{2,1,0:T(8,128)S(1)} %select_select_fusion.sl_ref, f32[8192,1536]{1,0:T(8,128)} %bitcast.60, ...), custom_call_target="tpu_custom_call", output_to_operand_aliasing={{0}: (6, {})} | custom-call | flops 25804800000 | bytes 40000000 | tf_op jit(solution)/shard_map/grad_w_840/pallas_call | solution.py:79
  306.9 1.4 collective-permute-start.9
  308.3 0.1 collective-permute-start.8
  308.4 0.4 collective-permute-start.2
  308.8 12.1 %collective-permute-done.refs_0_ = f32[384,1536]{1,0:T(8,128)} collective-permute-done((f32[384,1536]{1,0:T(8,128)}, f32[384,1536]{1,0:T(8,128)}, u32[]{:S(2)}, u32[]{:S(2)}) %collective-permute-start) | collective-permute-done | bytes 2359328 | tf_op jit(solution)/shard_map/ppermute | solution.py:556
  321.0 0.8 collective-permute-start.3
  321.8 1.4 collective-permute-done.1.refs_1_
  323.2 2.1 collective-permute-start.12
  325.3 2.0 collective-permute-done.2.refs_2_
  327.2 1.4 copy-done
  328.6 0.4 collective-permute-start.13
  329.0 1.6 collective-permute-done.3.refs_3_
  330.6 1.5 copy-done.2
  332.1 0.4 collective-permute-start.10
  332.5 1.5 collective-permute-done.12.refs_12_
  334.0 1.4 copy-done.11
  335.4 0.4 collective-permute-start.11
  335.8 0.7 fusion.9
  344.3 1.7 copy-done.1
  345.9 1.7 copy-done.3
  347.6 24.9 %place_14.1 = f32[9496,1536]{1,0:T(8,128)} custom-call(s32[14]{0:T(128)S(1)} %stack.99.where, f32[384,1536]{1,0:T(8,128)} %collective-permute-done.refs_0_, f32[384,1536]{1,0:T(8,128)} %collective-permute-done.1.refs_1_, f32[384,1536]{1,0:T(8,128)S(1)} %copy-done.1, f32[384,1536]{1,0:T(8,128)S(1)} %copy-done.3, ...), custom_call_target="tpu_custom_call", output_to_operand_aliasing={{}: (15, {})} | custom-call | flops 10000000000 | bytes 80000000 | tf_op jit(solution)/shard_map/place_14/pallas_call | solution.py:488
  372.5 5.1 %multiply_reduce_fusion = (f32[1536]{0:T(1024)S(1)}, f32[1024]{0:T(1024)S(1)}) fusion(f32[1024,1536]{1,0:T(8,128)} %all-reduce.2.cloned.1.call-done, bf16[2,512,1536]{2,1,0:T(8,128)(2,1)} %param.7, f32[1024]{0:T(1024)S(1)} %bitcast.70, f32[1536]{0:T(1024)S(1)} %copy-done.13), kind=kLoop, calls=%fused_computation.2 | loop fusion | flops 11007488 | bytes 9457664 | tf_op jit(solution)/shard_map/reduce_sum | solution.py:581
  377.7 0.8 collective-permute-start.14
  378.5 3.4 collective-permute-start.15
  381.9 0.3 collective-permute-start.16
  382.2 0.7 collective-permute-done.15
  383.0 1.4 collective-permute-done.16
  384.4 2.0 collective-permute-start.17
  386.4 2.7 multiply_convert_fusion
  389.2 0.6 add_reduce_fusion
  (66 shorter events, 1.3 us)
Async XLA Ops:
  7.2 8.6 %copy-start.8 = (bf16[2,512,1536]{2,1,0:T(8,128)(2,1)S(1)}, bf16[2,512,1536]{2,1,0:T(8,128)(2,1)}, u32[]{:S(2)}) copy-start(bf16[2,512,1536]{2,1,0:T(8,128)(2,1)} %param.7) | copy-start | bytes 9437188
  7.2 8.6 %copy-start.12 = (f32[1536]{0:T(1024)S(1)}, f32[1536]{0:T(1024)}, u32[]{:S(2)}) copy-start(f32[1536]{0:T(1024)} %param.8) | copy-start | bytes 18436
  7.2 365.3 %all-reduce.2.cloned.1.call-start = ((), (), s32[]{:S(2)}) async-start(), calls=%async_computation | async-start | bytes 12582912 | tf_op jit(solution)/shard_map/psum | solution.py:576
  10.0 9.2 %copy-start.15 = (f32[1,4,2,128]{3,1,2,0:T(4,128)}, f32[1,4,2,128]{3,1,2,0:T(4,128)S(1)}, u32[]{:S(2)}) copy-start(f32[1,4,2,128]{3,1,2,0:T(4,128)S(1)} %copy.18) | copy-start | bytes 12292
  142.8 0.8 copy-start.14
  142.8 5.2 %copy-start.17 = (f32[2,16]{1,0:T(2,128)S(1)}, f32[2,16]{1,0:T(2,128)}, u32[]{:S(2)}) copy-start(f32[2,16]{1,0:T(2,128)} %constant.128.clone.1) | copy-start | bytes 388
  181.0 1.4 copy-start.4
  182.4 1.4 copy-start.6
  217.5 52.9 %collective-permute-start.4 = (f32[384,1536]{1,0:T(8,128)}, f32[384,1536]{1,0:T(8,128)S(1)}, u32[]{:S(2)}, u32[]{:S(2)}) collective-permute-start(f32[384,1536]{1,0:T(8,128)} %get-tuple-element.28), channel_id=1, source_target_pairs={{0,6},{2,0},{4,2},{6,4},{1,7},{3,1},{5,3},{7,5},{8,14},{10,8},{12,... | collective-permute-start | bytes 7077896 | tf_op jit(solution)/shard_map/ppermute | solution.py:556
  217.6 90.7 %collective-permute-start.6 = (f32[384,1536]{1,0:T(8,128)}, f32[384,1536]{1,0:T(8,128)}, u32[]{:S(2)}, u32[]{:S(2)}) collective-permute-start(f32[384,1536]{1,0:T(8,128)} %get-tuple-element.28), channel_id=1, source_target_pairs={{0,1},{1,0},{2,3},{3,2},{4,5},{5,4},{6,7},{7,6},{8,9},{9,8},{10,11... | collective-permute-start | bytes 7077896 | tf_op jit(solution)/shard_map/ppermute | solution.py:563
  217.7 89.2 %collective-permute-start.5 = (f32[384,1536]{1,0:T(8,128)}, f32[384,1536]{1,0:T(8,128)}, u32[]{:S(2)}, u32[]{:S(2)}) collective-permute-start(f32[384,1536]{1,0:T(8,128)} %get-tuple-element.29), channel_id=1, source_target_pairs={{0,2},{2,4},{4,6},{6,0},{1,3},{3,5},{5,7},{7,1},{8,10},{10,12},{12... | collective-permute-start | bytes 7077896 | tf_op jit(solution)/shard_map/ppermute | solution.py:557
  219.4 89.0 %collective-permute-start.7 = (f32[384,1536]{1,0:T(8,128)}, f32[384,1536]{1,0:T(8,128)}, u32[]{:S(2)}, u32[]{:S(2)}) collective-permute-start(f32[384,1536]{1,0:T(8,128)} %get-tuple-element.29), channel_id=1, source_target_pairs={{0,1},{1,0},{2,3},{3,2},{4,5},{5,4},{6,7},{7,6},{8,9},{9,8},{10,11... | collective-permute-start | bytes 7077896 | tf_op jit(solution)/shard_map/ppermute | solution.py:563
  219.8 101.1 %collective-permute-start = (f32[384,1536]{1,0:T(8,128)}, f32[384,1536]{1,0:T(8,128)}, u32[]{:S(2)}, u32[]{:S(2)}) collective-permute-start(f32[384,1536]{1,0:T(8,128)} %copy-done.6), channel_id=1, source_target_pairs={{0,6},{2,0},{4,2},{6,4},{1,7},{3,1},{5,3},{7,5},{8,14},{10,8},{12,... | collective-permute-start | bytes 7077896 | tf_op jit(solution)/shard_map/ppermute | solution.py:556
  221.3 49.1 %copy-start.5 = (f32[384,1536]{1,0:T(8,128)S(1)}, f32[384,1536]{1,0:T(8,128)}, u32[]{:S(2)}) copy-start(f32[384,1536]{1,0:T(8,128)} %copy-done.4) | copy-start | bytes 7077892
  270.4 52.8 %collective-permute-start.1 = (f32[384,1536]{1,0:T(8,128)S(1)}, f32[384,1536]{1,0:T(8,128)}, u32[]{:S(2)}, u32[]{:S(2)}) collective-permute-start(f32[384,1536]{1,0:T(8,128)S(1)} %copy-done.5), channel_id=1, source_target_pairs={{0,2},{2,4},{4,6},{6,0},{1,3},{3,5},{5,7},{7,1},{8,10},{10,12},{12... | collective-permute-start | bytes 7077896 | tf_op jit(solution)/shard_map/ppermute | solution.py:557
  270.4 38.0 %copy-start.7 = (f32[384,1536]{1,0:T(8,128)S(1)}, f32[384,1536]{1,0:T(8,128)}, u32[]{:S(2)}) copy-start(f32[384,1536]{1,0:T(8,128)} %copy-done.6) | copy-start | bytes 7077892
  306.9 37.3 %collective-permute-start.9 = (f32[840,1536]{1,0:T(8,128)}, f32[840,1536]{1,0:T(8,128)}, u32[]{:S(2)}, u32[]{:S(2)}) collective-permute-start(f32[840,1536]{1,0:T(8,128)} %get-tuple-element.33), channel_id=1, source_target_pairs={{0,1},{1,0},{2,3},{3,2},{4,5},{5,4},{6,7},{7,6},{8,9},{9,8},{10,11... | collective-permute-start | bytes 15482888 | tf_op jit(solution)/shard_map/ppermute | solution.py:569
  308.3 35.9 %collective-permute-start.8 = (f32[840,1536]{1,0:T(8,128)}, f32[840,1536]{1,0:T(8,128)}, u32[]{:S(2)}, u32[]{:S(2)}) collective-permute-start(f32[840,1536]{1,0:T(8,128)} %get-tuple-element.31), channel_id=1, source_target_pairs={{0,1},{1,0},{2,3},{3,2},{4,5},{5,4},{6,7},{7,6},{8,9},{9,8},{10,11... | collective-permute-start | bytes 15482888 | tf_op jit(solution)/shard_map/ppermute | solution.py:569
  308.4 18.8 %collective-permute-start.2 = (f32[384,1536]{1,0:T(8,128)S(1)}, f32[384,1536]{1,0:T(8,128)S(1)}, u32[]{:S(2)}, u32[]{:S(2)}) collective-permute-start(f32[384,1536]{1,0:T(8,128)S(1)} %copy-done.7), channel_id=1, source_target_pairs={{0,1},{1,0},{2,3},{3,2},{4,5},{5,4},{6,7},{7,6},{8,9},{9,8},{10,11... | collective-permute-start | bytes 7077896 | tf_op jit(solution)/shard_map/ppermute | solution.py:563
  321.0 9.6 %collective-permute-start.3 = (f32[384,1536]{1,0:T(8,128)S(1)}, f32[384,1536]{1,0:T(8,128)S(1)}, u32[]{:S(2)}, u32[]{:S(2)}) collective-permute-start(f32[384,1536]{1,0:T(8,128)S(1)} %copy-done.5), channel_id=1, source_target_pairs={{0,1},{1,0},{2,3},{3,2},{4,5},{5,4},{6,7},{7,6},{8,9},{9,8},{10,11... | collective-permute-start | bytes 7077896 | tf_op jit(solution)/shard_map/ppermute | solution.py:563
  323.2 10.8 %collective-permute-start.12 = (f32[384,1536]{1,0:T(8,128)S(1)}, f32[384,1536]{1,0:T(8,128)S(1)}, u32[]{:S(2)}, u32[]{:S(2)}) collective-permute-start(f32[384,1536]{1,0:T(8,128)S(1)} %collective-permute-done.4.refs_4_), channel_id=1, source_target_pairs={{0,1},{1,0},{2,3},{3,2},{4,5},{5,4},{6,7},{7,6},{8,9},{9,8},{10,11... | collective-permute-start | bytes 7077896 | tf_op jit(solution)/shard_map/ppermute | solution.py:572
  327.2 1.4 copy-start
  328.6 15.6 %collective-permute-start.13 = (f32[384,1536]{1,0:T(8,128)}, f32[384,1536]{1,0:T(8,128)}, u32[]{:S(2)}, u32[]{:S(2)}) collective-permute-start(f32[384,1536]{1,0:T(8,128)} %collective-permute-done.5.refs_5_), channel_id=1, source_target_pairs={{0,1},{1,0},{2,3},{3,2},{4,5},{5,4},{6,7},{7,6},{8,9},{9,8},{10,11... | collective-permute-start | bytes 7077896 | tf_op jit(solution)/shard_map/ppermute | solution.py:572
  330.6 1.5 copy-start.2
  332.1 12.1 %collective-permute-start.10 = (f32[384,1536]{1,0:T(8,128)}, f32[384,1536]{1,0:T(8,128)}, u32[]{:S(2)}, u32[]{:S(2)}) collective-permute-start(f32[384,1536]{1,0:T(8,128)} %collective-permute-done.refs_0_), channel_id=1, source_target_pairs={{0,1},{1,0},{2,3},{3,2},{4,5},{5,4},{6,7},{7,6},{8,9},{9,8},{10,11... | collective-permute-start | bytes 7077896 | tf_op jit(solution)/shard_map/ppermute | solution.py:572
  334.0 1.4 copy-start.11
  335.4 8.8 %collective-permute-start.11 = (f32[384,1536]{1,0:T(8,128)}, f32[384,1536]{1,0:T(8,128)}, u32[]{:S(2)}, u32[]{:S(2)}) collective-permute-start(f32[384,1536]{1,0:T(8,128)} %collective-permute-done.1.refs_1_), channel_id=1, source_target_pairs={{0,1},{1,0},{2,3},{3,2},{4,5},{5,4},{6,7},{7,6},{8,9},{9,8},{10,11... | collective-permute-start | bytes 7077896 | tf_op jit(solution)/shard_map/ppermute | solution.py:572
  344.2 1.7 copy-start.1
  345.9 1.7 copy-start.3
  347.6 24.9 %copy-start.13 = (f32[1536]{0:T(1024)S(1)}, f32[1536]{0:T(1024)}, u32[]{:S(2)}) copy-start(f32[1536]{0:T(1024)} %param.8) | copy-start | bytes 18436
  347.6 24.9 %copy-start.16 = (f32[1,4,2,128]{3,1,2,0:T(4,128)S(1)}, f32[1,4,2,128]{3,1,2,0:T(4,128)}, u32[]{:S(2)}) copy-start(f32[1,4,2,128]{3,1,2,0:T(4,128)} %copy-done.15) | copy-start | bytes 12292
  372.5 13.9 %copy-start.9 = (bf16[2,512,1536]{2,1,0:T(8,128)(2,1)S(1)}, bf16[2,512,1536]{2,1,0:T(8,128)(2,1)}, u32[]{:S(2)}) copy-start(bf16[2,512,1536]{2,1,0:T(8,128)(2,1)} %param.7) | copy-start | bytes 9437188
  372.5 13.9 %copy-start.10 = (f32[1024,1536]{1,0:T(8,128)S(1)}, f32[1024,1536]{1,0:T(8,128)}, u32[]{:S(2)}) copy-start(f32[1024,1536]{1,0:T(8,128)} %all-reduce.2.cloned.1.call-done) | copy-start | bytes 18874372
  377.7 4.5 %collective-permute-start.14 = (f32[1,1536]{1,0:T(1,128)S(1)}, f32[1,1536]{1,0:T(1,128)S(1)}, u32[]{:S(2)}, u32[]{:S(2)}) collective-permute-start(f32[1,1536]{1,0:T(1,128)S(1)} %broadcast_in_dim.109), channel_id=1, source_target_pairs={{0,2},{2,4},{4,6},{6,0},{1,3},{3,5},{5,7},{7,1},{8,10},{10,12},{12... | collective-permute-start | bytes 18440 | tf_op jit(solution)/shard_map/ppermute | solution.py:582
  378.5 4.5 %collective-permute-start.15 = (f32[1,1536]{1,0:T(1,128)S(1)}, f32[1,1536]{1,0:T(1,128)S(1)}, u32[]{:S(2)}, u32[]{:S(2)}) collective-permute-start(f32[1,1536]{1,0:T(1,128)S(1)} %broadcast_in_dim.109), channel_id=1, source_target_pairs={{0,4},{2,6},{4,0},{6,2},{1,5},{3,7},{5,1},{7,3},{8,12},{10,14},{12... | collective-permute-start | bytes 18440 | tf_op jit(solution)/shard_map/ppermute | solution.py:582
  381.9 2.5 collective-permute-start.16
  384.4 4.7 %collective-permute-start.17 = (f32[1,1536]{1,0:T(1,128)S(1)}, f32[1,1536]{1,0:T(1,128)S(1)}, u32[]{:S(2)}, u32[]{:S(2)}) collective-permute-start(f32[1,1536]{1,0:T(1,128)S(1)} %fusion.4), channel_id=1, source_target_pairs={{0,1},{1,0},{2,3},{3,2},{4,5},{5,4},{6,7},{7,6},{8,9},{9,8},{10,11... | collective-permute-start | bytes 18440 | tf_op jit(solution)/shard_map/ppermute | solution.py:586
Sparse Core Ops, SparseCore 0:
  220.0 119.0 all-reduce.1
